TPU v7x, 32 devices: a whole 2x2x4 slice. The times are simulated.
32 devices in a mesh: row: 4 (over y, x), col: 8 (over z, core).
Axes of the slice: x: 2, y: 2, z: 4, core: 2. Of those that a mesh axis runs over, the one named last changes fastest.
Arguments:
- object_field: float32 [2, 1024, 2048], P(None, 'row', 'col'), may hold values from -40 to 40
- probe: float32 [2, 4, 256, 256], replicated, may hold values from -3 to 3
- pos_rows: int32 [4, 8, 2, 3], P('row', 'col'), may hold values from 0 to 255
- pos_cols: int32 [4, 8, 2, 3], P('row', 'col'), may hold values from 0 to 255
- counts: int32 [4, 8, 2], P('row', 'col'), may hold values from 1 to 3, as said below
- magnitudes: float32 [4, 8, 2, 3, 256, 256], P('row', 'col'), may hold values from 0 to 4
Outputs:
- object_out: float32 [2, 1024, 2048], P(None, 'row', 'col')
- probe_out: float32 [2, 4, 256, 256], replicated
- errors: float32 [4], replicated
Inputs may be any that keep to these rules, and one draw needn't show every extreme that they name: `counts`: every tile holds at least one live position in each batch, and in every batch some tile holds 3.
All inputs are finite; a program needn't handle non-finite values.
Results may differ from a plain program's by a relative error of at most 0.0015.
Values sent between devices are 32-bit elements; how exact they have to be, the bound alone decides.
A program may use at most 128 MiB of HBM per device.

v0:
```python
import functools
import math

import jax
import jax.numpy as jnp
import numpy as np
from jax import lax
from jax.experimental import pallas as pl
from jax.experimental.pallas import tpu as pltpu
from jax.sharding import PartitionSpec as P

BATCHES = 2
ITERS = 2


object_rate = 0.9
probe_rate = 0.5
floor_value = 0.5
tiny_value = 1e-06

CHUNK = 64
LANES = 128
SUBLANES = 8


def shifted(value, axis, steps):
    count = lax.axis_size(axis)
    leading, last = (max(0, -steps), min(count, count - steps))
    return lax.ppermute(value, axis, [(source, source + steps) for source in range(leading, last)])


def padded(array, sides, width):
    for axis, dim in sides:
        length = array.shape[dim]
        last = lax.slice_in_dim(array, length - width, length, axis=dim)
        leading = lax.slice_in_dim(array, 0, width, axis=dim)
        before = shifted(last, axis, 1)
        after = shifted(leading, axis, -1)
        array = jnp.concatenate([before, array, after], axis=dim)
    return array


def dft_tables(side):
    index = np.arange(side)
    angles = (index[:, None] * index[None, :] % side) * (2.0 * math.pi / side)
    cosine = np.cos(angles) / math.sqrt(side)
    sine = np.sin(angles) / math.sqrt(side)
    forward_left = np.block([[cosine, sine], [-sine, cosine]])
    inverse_left = np.block([[cosine, -sine], [sine, cosine]])
    return (jnp.asarray(forward_left, jnp.bfloat16), jnp.asarray(inverse_left, jnp.bfloat16))


def batch_kernel(
    rows_ref, cols_ref, count_ref, ext_ref, probe_ref, mag_ref, fwd_ref, inv_ref,
    grad_ref, sums_ref, win, far, term, square,
):
    modes, side = probe_ref.shape[1], probe_ref.shape[2]
    wide, tall = side + LANES, CHUNK + SUBLANES
    tail = 2 * modes * side

    grad_ref[...] = jnp.zeros_like(grad_ref)
    sums_ref[...] = jnp.zeros_like(sums_ref)

    def visit(slot, carry):
        row, col = rows_ref[slot], cols_ref[slot]
        first = pl.multiple_of(row // SUBLANES * SUBLANES, SUBLANES)
        down = row - first
        block = pl.multiple_of(col // LANES * LANES, LANES)
        offset = col - block

        for comp in range(2):
            for start in range(0, side, CHUNK):
                piece = ext_ref[comp, pl.ds(first + start, tall), pl.ds(block, wide)]
                piece = pltpu.roll(piece, lax.rem(wide - offset, wide), 1)[:, :side]
                piece = pltpu.roll(piece, lax.rem(tall - down, tall), 0)[:CHUNK]
                win[comp, start : start + CHUNK, :] = piece
                power = jnp.sum(piece * piece, axis=0, keepdims=True)
                sums_ref[tail : tail + 1, :] += power

        for mode in range(modes):
            p_re, p_im = probe_ref[0, mode], probe_ref[1, mode]
            w_re, w_im = win[0], win[1]
            wave = jnp.concatenate(
                [
                    (p_re * w_re - p_im * w_im).astype(jnp.bfloat16),
                    (p_re * w_im + p_im * w_re).astype(jnp.bfloat16),
                ],
                axis=0,
            )
            half = jnp.dot(fwd_ref[...], wave, preferred_element_type=jnp.float32).astype(jnp.bfloat16)
            half = jnp.concatenate([half[:side], half[side:]], axis=1)
            field = jnp.dot(half, inv_ref[...], preferred_element_type=jnp.float32)
            far[mode] = field
            norm = field[:, :side] * field[:, :side] + field[:, side:] * field[:, side:]
            if mode == 0:
                square[...] = norm
            else:
                square[...] += norm

        for start in range(0, side, CHUNK):
            span = slice(start, start + CHUNK)
            modulus = jnp.sqrt(square[span, :])
            amplitude = mag_ref[slot, span, :]
            miss = modulus - amplitude
            sums_ref[tail + 1 : tail + 2, :] += jnp.sum(miss * miss, axis=0, keepdims=True)
            square[span, :] = amplitude / jnp.maximum(modulus, floor_value) - 1.0

        for mode in range(modes):
            factor = square[...]
            fix = jnp.concatenate(
                [
                    (far[mode, :, :side] * factor).astype(jnp.bfloat16),
                    (far[mode, :, side:] * factor).astype(jnp.bfloat16),
                ],
                axis=0,
            )
            half = jnp.dot(inv_ref[...], fix, preferred_element_type=jnp.float32).astype(jnp.bfloat16)
            half = jnp.concatenate([half[:side], half[side:]], axis=1)
            wave = jnp.dot(half, fwd_ref[...], preferred_element_type=jnp.float32)
            u_re, u_im = wave[:, :side], wave[:, side:]
            p_re, p_im = probe_ref[0, mode], probe_ref[1, mode]
            w_re, w_im = win[0], win[1]
            t_re = p_re * u_re + p_im * u_im
            t_im = p_re * u_im - p_im * u_re
            if mode == 0:
                term[0, :, :side] = t_re
                term[1, :, :side] = t_im
            else:
                term[0, :, :side] += t_re
                term[1, :, :side] += t_im
            at_re, at_im = mode * side, (modes + mode) * side
            sums_ref[at_re : at_re + side, :] += w_re * u_re + w_im * u_im
            sums_ref[at_im : at_im + side, :] += w_re * u_im - w_im * u_re

        for comp in range(2):
            for start in range(0, side, CHUNK):
                piece = term[comp, start : start + CHUNK, :]
                piece = pltpu.roll(piece, offset, 1)
                piece = jnp.concatenate([piece, jnp.zeros((SUBLANES, wide), jnp.float32)], axis=0)
                piece = pltpu.roll(piece, down, 0)
                grad_ref[comp, pl.ds(first + start, tall), pl.ds(block, wide)] += piece
        return carry

    term[:, :, side:] = jnp.zeros((2, side, LANES), jnp.float32)
    lax.fori_loop(0, count_ref[0], visit, 0)


def batch_sums(extended, probe, rows, cols, count, magnitudes, forward, inverse):
    modes, side = probe.shape[1], probe.shape[2]
    vmem = pl.BlockSpec(memory_space=pltpu.VMEM)
    smem = pl.BlockSpec(memory_space=pltpu.SMEM)
    flops = 2 * magnitudes.shape[0] * modes * 4 * 2 * side * side * 4 * side
    return pl.pallas_call(
        batch_kernel,
        out_shape=(
            jax.ShapeDtypeStruct(extended.shape, jnp.float32),
            jax.ShapeDtypeStruct((2 * modes * side + 8, side), jnp.float32),
        ),
        in_specs=[smem] * 3 + [vmem] * 5,
        out_specs=(vmem, vmem),
        scratch_shapes=[
            pltpu.VMEM((2, side, side), jnp.float32),
            pltpu.VMEM((modes, side, 2 * side), jnp.float32),
            pltpu.VMEM((2, side, side + LANES), jnp.float32),
            pltpu.VMEM((side, side), jnp.float32),
        ],
        compiler_params=pltpu.CompilerParams(vmem_limit_bytes=32 * 2**20),
        cost_estimate=pl.CostEstimate(flops=flops, bytes_accessed=10 * 2**20, transcendentals=0),
    )(rows, cols, count, extended, probe, magnitudes, forward, inverse)


def return_rims(object_grad, margin):
    from_left = shifted(object_grad[:, :, -margin:], "col", 1)
    from_right = shifted(object_grad[:, :, :margin], "col", -1)
    middle = object_grad[:, :, margin:-margin] + jnp.concatenate([from_left, from_right], axis=2)
    from_above = shifted(middle[:, -margin:, :], "row", 1)
    from_below = shifted(middle[:, :margin, :], "row", -1)
    return middle[:, margin:-margin, :] + jnp.concatenate([from_above, from_below], axis=1)


def on_device(object_field, probe, pos_rows, pos_cols, counts, magnitudes):
    modes, side = probe.shape[1], probe.shape[2]
    margin = side // 2
    forward, inverse = dft_tables(side)
    errors = []
    for sweep in range(ITERS):
        for batch in range(BATCHES):
            extended = padded(object_field, (("row", 1), ("col", 2)), margin)
            object_grad, sums = batch_sums(
                extended, probe, pos_rows[0, 0, batch], pos_cols[0, 0, batch], counts[0, 0, batch : batch + 1],
                magnitudes[0, 0, batch], forward, inverse,
            )
            probe_peak = jnp.max(jnp.sum(probe * probe, axis=(0, 1))) + tiny_value
            total = lax.psum(sums, ("row", "col"))
            interior = return_rims(object_grad, margin)
            object_field = object_field + object_rate / probe_peak * interior
            tail = 2 * modes * side
            power_total = jnp.sum(total[tail])
            errors.append(jnp.sum(total[tail + 1]))
            summed = total[:tail].reshape(probe.shape)
            probe = probe + probe_rate * side * side / power_total * summed
    return (object_field, probe, jnp.stack(errors))


def solution(mesh):
    return jax.shard_map(
        on_device,
        mesh=mesh,
        in_specs=(
            P(None, "row", "col"),
            P(),
            P("row", "col", None, None),
            P("row", "col", None, None),
            P("row", "col", None),
            P("row", "col", None, None, None, None),
        ),
        out_specs=(P(None, "row", "col"), P(), P()),
        check_vma=False,
    )
```

profile of v0, /device:TPU:0, one launch (start us, length us, event | category | flops | bytes accessed | tf_op | source)
XLA Modules:
  0.0 757.7 jit_solution(16915535525950174074)
XLA Ops:
  8.3 4.9 collective-permute-start
  13.2 1.4 collective-permute-start.1
  14.7 4.1 collective-permute-done
  19.8 6.5 collective-permute-done.1
  26.4 1.3 collective-permute-start.2
  29.8 3.5 collective-permute-done.3
  33.6 7.6 shard_map.103
  41.3 9.1 %collective-permute-start.4 = (f32[2,512,128]{2,1,0:T(8,128)S(1)}, f32[2,512,128]{2,1,0:T(8,128)S(1)}, u32[]{:S(2)}, u32[]{:S(2)}) collective-permute-start(f32[2,512,128]{2,1,0:T(8,128)S(1)} %get-tuple-element.40), channel_id=1, source_target_pairs={{0,1},{1,2},{2,3},{3,4},{4,5},{5,6},{6,7},{8,9},{9,10},{10,11},{11... | collective-permute-start | bytes 1572872 | tf_op jit(solution)/shard_map/ppermute | solution.py:29
  51.9 2.3 collective-permute-done.5
  56.2 13.1 %collective-permute-start.6 = (f32[2,128,256]{2,1,0:T(8,128)}, f32[2,128,256]{2,1,0:T(8,128)}, u32[]{:S(2)}, u32[]{:S(2)}) collective-permute-start(f32[2,128,256]{2,1,0:T(8,128)} %get-tuple-element.56), channel_id=1, source_target_pairs={{0,8},{8,16},{16,24},{1,9},{9,17},{17,25},{2,10},{10,18},{18,26},{... | collective-permute-start | bytes 786440 | tf_op jit(solution)/shard_map/ppermute | solution.py:29
  70.6 121.3 %all-reduce.5.cloned.1.call-done = f32[2056,256]{1,0:T(8,128)} async-done(((f32[2056,256]{1,0:T(8,128)}), f32[2056,256]{1,0:T(8,128)}) %all-reduce.5.cloned.1.call-update) | async-done | bytes 2105360 | tf_op jit(solution)/shard_map/psum | solution.py:194
  191.9 1.4 slice_reduce_fusion.3
  194.0 1.9 slice_multiply_fusion.3
  197.4 1.8 reduce_max.36
  199.9 1.4 fusion.7
  201.4 3.4 collective-permute-start.8
  206.1 4.1 collective-permute-done.8
  210.3 7.5 collective-permute-done.9
  217.9 1.3 collective-permute-start.10
  219.3 1.4 collective-permute-start.11
  220.7 3.0 collective-permute-done.11
  223.9 15.2 %shard_map.104 = (f32[2,512,512]{2,1,0:T(8,128)S(1)}, f32[2056,256]{1,0:T(8,128)S(1)}) custom-call(s32[3]{0:T(128)S(1)} %get-tuple-element.75.rows_ref, s32[3]{0:T(128)S(1)} %get-tuple-element.68.cols_ref, s32[1]{0:T(128)} %bitcast.7.count_ref, f32[2,512,512]{2,1,0:T(8,128)S(1)} %pad_maximum_fusion.1.ext_ref, ...), custom_call_target="tpu_custom_call" | custom-call | flops 12884901888 | bytes 10485760 | tf_op jit(solution)/shard_map/pallas_call | solution.py:153
  239.2 4.6 collective-permute-start.12
  243.8 1.4 collective-permute-start.13
  245.3 2.5 collective-permute-done.13
  248.8 7.1 collective-permute-start.14
  258.6 1.4 collective-permute-done.14
  260.0 4.4 collective-permute-done.15
  265.6 5.2 collective-permute-start.16
  272.1 5.0 collective-permute-done.16
  277.1 7.4 collective-permute-done.17
  285.7 5.4 collective-permute-start.18
  292.4 106.4 %all-reduce.7.cloned.1.call-done = f32[2056,256]{1,0:T(8,128)} async-done(((f32[2056,256]{1,0:T(8,128)}), f32[2056,256]{1,0:T(8,128)}) %all-reduce.7.cloned.1.call-update) | async-done | bytes 2105360 | tf_op jit(solution)/shard_map/psum | solution.py:194
  398.8 1.4 slice_reduce_fusion.2
  400.8 1.9 slice_multiply_fusion.2
  404.2 1.5 pad_maximum_fusion.2.ext_ref
  405.7 6.0 shard_map.105
  411.8 1.6 collective-permute-start.20
  414.9 4.5 collective-permute-done.21
  420.8 13.1 %collective-permute-start.22 = (f32[2,128,256]{2,1,0:T(8,128)}, f32[2,128,256]{2,1,0:T(8,128)}, u32[]{:S(2)}, u32[]{:S(2)}) collective-permute-start(f32[2,128,256]{2,1,0:T(8,128)} %get-tuple-element.48), channel_id=1, source_target_pairs={{0,8},{8,16},{16,24},{1,9},{9,17},{17,25},{2,10},{10,18},{18,26},{... | collective-permute-start | bytes 786440 | tf_op jit(solution)/shard_map/ppermute | solution.py:29
  435.1 1.6 reduce_max.38
  437.4 5.0 collective-permute-done.23
  442.4 1.4 fusion.3
  443.9 4.8 collective-permute-start.24
  448.7 1.5 collective-permute-start.25
  450.2 3.4 collective-permute-done.24
  453.6 9.3 %collective-permute-done.25 = f32[2,128,256]{2,1,0:T(8,128)S(1)} collective-permute-done((f32[2,128,256]{2,1,0:T(8,128)S(1)}, f32[2,128,256]{2,1,0:T(8,128)S(1)}, u32[]{:S(2)}, u32[]{:S(2)}) %collective-permute-start.25) | collective-permute-done | bytes 262176 | tf_op jit(solution)/shard_map/ppermute | solution.py:29
  464.0 5.7 collective-permute-start.26
  471.0 106.6 %all-reduce.9.cloned.1.call-done = f32[2056,256]{1,0:T(8,128)} async-done(((f32[2056,256]{1,0:T(8,128)}), f32[2056,256]{1,0:T(8,128)}) %all-reduce.9.cloned.1.call-update) | async-done | bytes 2105360 | tf_op jit(solution)/shard_map/psum | solution.py:194
  577.6 1.4 slice_reduce_fusion.1
  579.7 1.7 slice_multiply_fusion.1
  582.6 2.2 pad_maximum_fusion.3.ext_ref
  584.8 16.9 %shard_map.106 = (f32[2,512,512]{2,1,0:T(8,128)S(1)}, f32[2056,256]{1,0:T(8,128)}) custom-call(s32[3]{0:T(128)S(1)} %get-tuple-element.75.rows_ref, s32[3]{0:T(128)S(1)} %get-tuple-element.68.cols_ref, s32[1]{0:T(128)} %bitcast.7.count_ref, f32[2,512,512]{2,1,0:T(8,128)S(1)} %pad_maximum_fusion.3.ext_ref, ...), custom_call_target="tpu_custom_call" | custom-call | flops 12884901888 | bytes 10485760 | tf_op jit(solution)/shard_map/pallas_call | solution.py:153
  602.8 1.3 collective-permute-start.28
  605.8 2.5 collective-permute-done.29
  610.5 5.8 collective-permute-start.30
  619.0 2.1 collective-permute-done.30
  621.1 4.2 collective-permute-done.31
  625.3 1.9 fusion.1
  627.3 114.7 %all-reduce.11.cloned.1.call-done = f32[2056,256]{1,0:T(8,128)} async-done(((f32[2056,256]{1,0:T(8,128)}), f32[2056,256]{1,0:T(8,128)}) %all-reduce.11.cloned.1.call-update) | async-done | bytes 2105360 | tf_op jit(solution)/shard_map/psum | solution.py:194
  742.0 1.5 slice_reduce_fusion
  744.1 1.9 slice_multiply_fusion
  746.4 1.7 add.87
  748.0 3.1 pad_maximum_fusion.7
  (148 shorter events, 37.2 us)
Async XLA Ops:
  7.2 184.7 %all-reduce.5.cloned.1.call-start = ((), (), s32[]{:S(2)}) async-start(), calls=%async_computation | async-start | bytes 4210688 | tf_op jit(solution)/shard_map/psum | solution.py:194
  8.3 10.4 %collective-permute-start = (f32[2,128,256]{2,1,0:T(8,128)S(1)}, f32[2,128,256]{2,1,0:T(8,128)S(1)}, u32[]{:S(2)}, u32[]{:S(2)}) collective-permute-start(f32[2,128,256]{2,1,0:T(8,128)S(1)} %get-tuple-element.67), channel_id=1, source_target_pairs={{0,8},{8,16},{16,24},{1,9},{9,17},{17,25},{2,10},{10,18},{18,26},{... | collective-permute-start | bytes 786440 | tf_op jit(solution)/shard_map/ppermute | solution.py:29
  13.2 15.8 %copy-start.36 = (s32[1,1,2]{2,1,0:T(1,128)S(1)}, s32[1,1,2]{2,1,0:T(1,128)}, u32[]{:S(2)}) copy-start(s32[1,1,2]{2,1,0:T(1,128)} %param.12) | copy-start | bytes 28
  13.2 16.4 %copy-start.37 = (s32[1,1,2,3]{3,2,1,0:T(2,128)S(1)}, s32[1,1,2,3]{3,2,1,0:T(2,128)}, u32[]{:S(2)}) copy-start(s32[1,1,2,3]{3,2,1,0:T(2,128)} %param.11) | copy-start | bytes 76
  13.2 16.4 %copy-start.38 = (s32[1,1,2,3]{3,2,1,0:T(2,128)S(1)}, s32[1,1,2,3]{3,2,1,0:T(2,128)}, u32[]{:S(2)}) copy-start(s32[1,1,2,3]{3,2,1,0:T(2,128)} %param.10) | copy-start | bytes 76
  13.2 16.4 %copy-start.25 = (f32[1,1,2,3,256,256]{5,4,3,2,1,0:T(8,128)S(1)}, f32[1,1,2,3,256,256]{5,4,3,2,1,0:T(8,128)}, u32[]{:S(2)}) copy-start(f32[1,1,2,3,256,256]{5,4,3,2,1,0:T(8,128)} %param.13) | copy-start | bytes 4718596
  13.2 13.0 %collective-permute-start.1 = (f32[2,128,256]{2,1,0:T(8,128)S(1)}, f32[2,128,256]{2,1,0:T(8,128)S(1)}, u32[]{:S(2)}, u32[]{:S(2)}) collective-permute-start(f32[2,128,256]{2,1,0:T(8,128)S(1)} %get-tuple-element.66), channel_id=1, source_target_pairs={{8,0},{16,8},{24,16},{9,1},{17,9},{25,17},{10,2},{18,10},{26,18},{... | collective-permute-start | bytes 786440 | tf_op jit(solution)/shard_map/ppermute | solution.py:29
  26.4 3.4 collective-permute-start.2
  27.7 5.6 collective-permute-start.3
  29.7 3.8 copy-start.8
  29.7 3.8 copy-start.6
  29.8 3.8 copy-start.10
  29.8 3.8 copy-start.11
  41.2 357.6 %all-reduce.7.cloned.1.call-start = ((), (), s32[]{:S(2)}) async-start(), calls=%async_computation.1 | async-start | bytes 4210688 | tf_op jit(solution)/shard_map/psum | solution.py:194
  41.3 10.6 %collective-permute-start.4 = (f32[2,512,128]{2,1,0:T(8,128)S(1)}, f32[2,512,128]{2,1,0:T(8,128)S(1)}, u32[]{:S(2)}, u32[]{:S(2)}) collective-permute-start(f32[2,512,128]{2,1,0:T(8,128)S(1)} %get-tuple-element.40), channel_id=1, source_target_pairs={{0,1},{1,2},{2,3},{3,4},{4,5},{5,6},{6,7},{8,9},{9,10},{10,11},{11... | collective-permute-start | bytes 1572872 | tf_op jit(solution)/shard_map/ppermute | solution.py:29
  50.4 3.8 collective-permute-start.5
  56.2 143.7 %collective-permute-start.6 = (f32[2,128,256]{2,1,0:T(8,128)}, f32[2,128,256]{2,1,0:T(8,128)}, u32[]{:S(2)}, u32[]{:S(2)}) collective-permute-start(f32[2,128,256]{2,1,0:T(8,128)} %get-tuple-element.56), channel_id=1, source_target_pairs={{0,8},{8,16},{16,24},{1,9},{9,17},{17,25},{2,10},{10,18},{18,26},{... | collective-permute-start | bytes 786440 | tf_op jit(solution)/shard_map/ppermute | solution.py:29
  69.3 130.6 %collective-permute-start.7 = (f32[2,128,256]{2,1,0:T(8,128)}, f32[2,128,256]{2,1,0:T(8,128)}, u32[]{:S(2)}, u32[]{:S(2)}) collective-permute-start(f32[2,128,256]{2,1,0:T(8,128)} %get-tuple-element.57), channel_id=1, source_target_pairs={{8,0},{16,8},{24,16},{9,1},{17,9},{25,17},{10,2},{18,10},{26,18},{... | collective-permute-start | bytes 786440 | tf_op jit(solution)/shard_map/ppermute | solution.py:29
  194.0 2.2 copy-start.7
  197.4 26.5 %copy-start.2 = (f32[2,4,256,256]{3,2,1,0:T(8,128)}, f32[2,4,256,256]{3,2,1,0:T(8,128)S(1)}, u32[]{:S(2)}) copy-start(f32[2,4,256,256]{3,2,1,0:T(8,128)S(1)} %get-tuple-element.32.probe_ref) | copy-start | bytes 6291460
  201.4 22.3 %copy-start.20 = (f32[2,256,256]{2,1,0:T(8,128)}, f32[2,256,256]{2,1,0:T(8,128)S(1)}, u32[]{:S(2)}) copy-start(f32[2,256,256]{2,1,0:T(8,128)S(1)} %fusion.7) | copy-start | bytes 1572868
  201.4 8.9 %collective-permute-start.8 = (f32[2,128,256]{2,1,0:T(8,128)S(1)}, f32[2,128,256]{2,1,0:T(8,128)S(1)}, u32[]{:S(2)}, u32[]{:S(2)}) collective-permute-start(f32[2,128,256]{2,1,0:T(8,128)S(1)} %get-tuple-element.64), channel_id=1, source_target_pairs={{0,8},{8,16},{16,24},{1,9},{9,17},{17,25},{2,10},{10,18},{18,26},{... | collective-permute-start | bytes 786440 | tf_op jit(solution)/shard_map/ppermute | solution.py:29
  204.8 12.9 %collective-permute-start.9 = (f32[2,128,256]{2,1,0:T(8,128)S(1)}, f32[2,128,256]{2,1,0:T(8,128)S(1)}, u32[]{:S(2)}, u32[]{:S(2)}) collective-permute-start(f32[2,128,256]{2,1,0:T(8,128)S(1)} %get-tuple-element.65), channel_id=1, source_target_pairs={{8,0},{16,8},{24,16},{9,1},{17,9},{25,17},{10,2},{18,10},{26,18},{... | collective-permute-start | bytes 786440 | tf_op jit(solution)/shard_map/ppermute | solution.py:29
  217.9 2.8 collective-permute-start.10
  219.2 4.7 copy-start.12
  219.3 4.4 collective-permute-start.11
  239.1 8.8 %copy-start.5 = (f32[2056,256]{1,0:T(8,128)}, f32[2056,256]{1,0:T(8,128)S(1)}, u32[]{:S(2)}) copy-start(f32[2056,256]{1,0:T(8,128)S(1)} %get-tuple-element.14) | copy-start | bytes 6316036
  239.2 6.1 collective-permute-start.12
  243.8 13.3 %copy-start.35 = (f32[256,256]{1,0:T(8,128)S(1)}, f32[256,256]{1,0:T(8,128)}, u32[]{:S(2)}) copy-start(f32[256,256]{1,0:T(8,128)} %get-tuple-element.31) | copy-start | bytes 786436
  243.8 3.9 collective-permute-start.13
  248.0 16.5 %copy-start.21 = (f32[2,256,256]{2,1,0:T(8,128)S(1)}, f32[2,256,256]{2,1,0:T(8,128)}, u32[]{:S(2)}) copy-start(f32[2,256,256]{2,1,0:T(8,128)} %copy-done.20) | copy-start | bytes 1572868
  248.8 11.2 %collective-permute-start.14 = (f32[2,128,256]{2,1,0:T(8,128)}, f32[2,128,256]{2,1,0:T(8,128)S(1)}, u32[]{:S(2)}, u32[]{:S(2)}) collective-permute-start(f32[2,128,256]{2,1,0:T(8,128)} %get-tuple-element.52), channel_id=1, source_target_pairs={{0,8},{8,16},{16,24},{1,9},{9,17},{17,25},{2,10},{10,18},{18,26},{... | collective-permute-start | bytes 786440 | tf_op jit(solution)/shard_map/ppermute | solution.py:29
  255.9 8.6 %collective-permute-start.15 = (f32[2,128,256]{2,1,0:T(8,128)}, f32[2,128,256]{2,1,0:T(8,128)}, u32[]{:S(2)}, u32[]{:S(2)}) collective-permute-start(f32[2,128,256]{2,1,0:T(8,128)} %get-tuple-element.53), channel_id=1, source_target_pairs={{8,0},{16,8},{24,16},{9,1},{17,9},{25,17},{10,2},{18,10},{26,18},{... | collective-permute-start | bytes 786440 | tf_op jit(solution)/shard_map/ppermute | solution.py:29
  258.6 319.0 %all-reduce.9.cloned.1.call-start = ((), (), s32[]{:S(2)}) async-start(), calls=%async_computation.2 | async-start | bytes 4210688 | tf_op jit(solution)/shard_map/psum | solution.py:194
  265.5 20.2 %copy-start.18 = (f32[2,256,256]{2,1,0:T(8,128)}, f32[2,256,256]{2,1,0:T(8,128)S(1)}, u32[]{:S(2)}) copy-start(f32[2,256,256]{2,1,0:T(8,128)S(1)} %fusion.5) | copy-start | bytes 1572868
  265.6 11.6 %collective-permute-start.16 = (f32[2,128,256]{2,1,0:T(8,128)S(1)}, f32[2,128,256]{2,1,0:T(8,128)S(1)}, u32[]{:S(2)}, u32[]{:S(2)}) collective-permute-start(f32[2,128,256]{2,1,0:T(8,128)S(1)} %get-tuple-element.62), channel_id=1, source_target_pairs={{0,8},{8,16},{16,24},{1,9},{9,17},{17,25},{2,10},{10,18},{18,26},{... | collective-permute-start | bytes 786440 | tf_op jit(solution)/shard_map/ppermute | solution.py:29
  270.8 13.8 %collective-permute-start.17 = (f32[2,128,256]{2,1,0:T(8,128)S(1)}, f32[2,128,256]{2,1,0:T(8,128)S(1)}, u32[]{:S(2)}, u32[]{:S(2)}) collective-permute-start(f32[2,128,256]{2,1,0:T(8,128)S(1)} %get-tuple-element.63), channel_id=1, source_target_pairs={{8,0},{16,8},{24,16},{9,1},{17,9},{25,17},{10,2},{18,10},{26,18},{... | collective-permute-start | bytes 786440 | tf_op jit(solution)/shard_map/ppermute | solution.py:29
  277.1 8.5 %copy-start.27 = (f32[2,128,256]{2,1,0:T(8,128)}, f32[2,128,256]{2,1,0:T(8,128)S(1)}, u32[]{:S(2)}) copy-start(f32[2,128,256]{2,1,0:T(8,128)S(1)} %collective-permute-done.16) | copy-start | bytes 786436
  285.7 118.4 %collective-permute-start.18 = (f32[2,512,128]{2,1,0:T(8,128)}, f32[2,512,128]{2,1,0:T(8,128)}, u32[]{:S(2)}, u32[]{:S(2)}) collective-permute-start(f32[2,512,128]{2,1,0:T(8,128)} %get-tuple-element.50), channel_id=1, source_target_pairs={{0,1},{1,2},{2,3},{3,4},{4,5},{5,6},{6,7},{8,9},{9,10},{10,11},{11... | collective-permute-start | bytes 1572872 | tf_op jit(solution)/shard_map/ppermute | solution.py:29
  291.1 113.0 %collective-permute-start.19 = (f32[2,512,128]{2,1,0:T(8,128)}, f32[2,512,128]{2,1,0:T(8,128)}, u32[]{:S(2)}, u32[]{:S(2)}) collective-permute-start(f32[2,512,128]{2,1,0:T(8,128)} %get-tuple-element.51), channel_id=1, source_target_pairs={{1,0},{2,1},{3,2},{4,3},{5,4},{6,5},{7,6},{9,8},{10,9},{11,10},{12... | collective-permute-start | bytes 1572872 | tf_op jit(solution)/shard_map/ppermute | solution.py:29
  400.8 2.2 copy-start.3
  404.0 1.7 copy-start.9
  404.0 1.7 copy-start.13
  411.7 7.9 %copy-start.4 = (f32[2056,256]{1,0:T(8,128)}, f32[2056,256]{1,0:T(8,128)S(1)}, u32[]{:S(2)}) copy-start(f32[2056,256]{1,0:T(8,128)S(1)} %get-tuple-element.16) | copy-start | bytes 6316036
  411.8 3.1 collective-permute-start.20
  413.4 6.0 collective-permute-start.21
  420.8 16.7 %collective-permute-start.22 = (f32[2,128,256]{2,1,0:T(8,128)}, f32[2,128,256]{2,1,0:T(8,128)}, u32[]{:S(2)}, u32[]{:S(2)}) collective-permute-start(f32[2,128,256]{2,1,0:T(8,128)} %get-tuple-element.48), channel_id=1, source_target_pairs={{0,8},{8,16},{16,24},{1,9},{9,17},{17,25},{2,10},{10,18},{18,26},{... | collective-permute-start | bytes 786440 | tf_op jit(solution)/shard_map/ppermute | solution.py:29
  433.8 8.6 %collective-permute-start.23 = (f32[2,128,256]{2,1,0:T(8,128)}, f32[2,128,256]{2,1,0:T(8,128)}, u32[]{:S(2)}, u32[]{:S(2)}) collective-permute-start(f32[2,128,256]{2,1,0:T(8,128)} %get-tuple-element.49), channel_id=1, source_target_pairs={{8,0},{16,8},{24,16},{9,1},{17,9},{25,17},{10,2},{18,10},{26,18},{... | collective-permute-start | bytes 786440 | tf_op jit(solution)/shard_map/ppermute | solution.py:29
  437.4 304.6 %all-reduce.11.cloned.1.call-start = ((), (), s32[]{:S(2)}) async-start(), calls=%async_computation.3 | async-start | bytes 4210688 | tf_op jit(solution)/shard_map/psum | solution.py:194
  443.9 20.1 %copy-start.15 = (f32[2,256,256]{2,1,0:T(8,128)}, f32[2,256,256]{2,1,0:T(8,128)S(1)}, u32[]{:S(2)}) copy-start(f32[2,256,256]{2,1,0:T(8,128)S(1)} %fusion.3) | copy-start | bytes 1572868
  443.9 9.7 %collective-permute-start.24 = (f32[2,128,256]{2,1,0:T(8,128)S(1)}, f32[2,128,256]{2,1,0:T(8,128)S(1)}, u32[]{:S(2)}, u32[]{:S(2)}) collective-permute-start(f32[2,128,256]{2,1,0:T(8,128)S(1)} %get-tuple-element.60), channel_id=1, source_target_pairs={{0,8},{8,16},{16,24},{1,9},{9,17},{17,25},{2,10},{10,18},{18,26},{... | collective-permute-start | bytes 786440 | tf_op jit(solution)/shard_map/ppermute | solution.py:29
  448.7 14.1 %collective-permute-start.25 = (f32[2,128,256]{2,1,0:T(8,128)S(1)}, f32[2,128,256]{2,1,0:T(8,128)S(1)}, u32[]{:S(2)}, u32[]{:S(2)}) collective-permute-start(f32[2,128,256]{2,1,0:T(8,128)S(1)} %get-tuple-element.61), channel_id=1, source_target_pairs={{8,0},{16,8},{24,16},{9,1},{17,9},{25,17},{10,2},{18,10},{26,18},{... | collective-permute-start | bytes 786440 | tf_op jit(solution)/shard_map/ppermute | solution.py:29
  453.6 10.4 %copy-start.29 = (f32[2,128,256]{2,1,0:T(8,128)}, f32[2,128,256]{2,1,0:T(8,128)S(1)}, u32[]{:S(2)}) copy-start(f32[2,128,256]{2,1,0:T(8,128)S(1)} %collective-permute-done.24) | copy-start | bytes 786436
  464.0 118.4 %collective-permute-start.26 = (f32[2,512,128]{2,1,0:T(8,128)}, f32[2,512,128]{2,1,0:T(8,128)}, u32[]{:S(2)}, u32[]{:S(2)}) collective-permute-start(f32[2,512,128]{2,1,0:T(8,128)} %get-tuple-element.46), channel_id=1, source_target_pairs={{0,1},{1,2},{2,3},{3,4},{4,5},{5,6},{6,7},{8,9},{9,10},{10,11},{11... | collective-permute-start | bytes 1572872 | tf_op jit(solution)/shard_map/ppermute | solution.py:29
  469.7 112.8 %collective-permute-start.27 = (f32[2,512,128]{2,1,0:T(8,128)}, f32[2,512,128]{2,1,0:T(8,128)}, u32[]{:S(2)}, u32[]{:S(2)}) collective-permute-start(f32[2,512,128]{2,1,0:T(8,128)} %get-tuple-element.47), channel_id=1, source_target_pairs={{1,0},{2,1},{3,2},{4,3},{5,4},{6,5},{7,6},{9,8},{10,9},{11,10},{12... | collective-permute-start | bytes 1572872 | tf_op jit(solution)/shard_map/ppermute | solution.py:29
  582.4 2.4 copy-start
  582.4 2.4 copy-start.14
  602.8 3.0 collective-permute-start.28
  604.1 4.1 collective-permute-start.29
  605.4 12.2 %copy-start.26 = (f32[256,256]{1,0:T(8,128)S(1)}, f32[256,256]{1,0:T(8,128)}, u32[]{:S(2)}) copy-start(f32[256,256]{1,0:T(8,128)} %get-tuple-element.27) | copy-start | bytes 786436
  605.4 19.9 %copy-start.17 = (f32[2,256,256]{2,1,0:T(8,128)S(1)}, f32[2,256,256]{2,1,0:T(8,128)}, u32[]{:S(2)}) copy-start(f32[2,256,256]{2,1,0:T(8,128)} %copy-done.15) | copy-start | bytes 1572868
  610.5 10.6 %collective-permute-start.30 = (f32[2,128,256]{2,1,0:T(8,128)S(1)}, f32[2,128,256]{2,1,0:T(8,128)S(1)}, u32[]{:S(2)}, u32[]{:S(2)}) collective-permute-start(f32[2,128,256]{2,1,0:T(8,128)S(1)} %get-tuple-element.44), channel_id=1, source_target_pairs={{0,8},{8,16},{16,24},{1,9},{9,17},{17,25},{2,10},{10,18},{18,26},{... | collective-permute-start | bytes 786440 | tf_op jit(solution)/shard_map/ppermute | solution.py:29
  616.3 9.0 %collective-permute-start.31 = (f32[2,128,256]{2,1,0:T(8,128)S(1)}, f32[2,128,256]{2,1,0:T(8,128)S(1)}, u32[]{:S(2)}, u32[]{:S(2)}) collective-permute-start(f32[2,128,256]{2,1,0:T(8,128)S(1)} %get-tuple-element.45), channel_id=1, source_target_pairs={{8,0},{16,8},{24,16},{9,1},{17,9},{25,17},{10,2},{18,10},{26,18},{... | collective-permute-start | bytes 786440 | tf_op jit(solution)/shard_map/ppermute | solution.py:29
  744.1 2.2 copy-start.1
  (11 other events, 12.0 us)
Sparse Core Ops, SparseCore 0:
  41.3 150.5 all-reduce.4
  258.7 140.0 all-reduce.6
  437.5 140.0 all-reduce.8
  605.5 136.4 all-reduce.10
where the time goes:
time: 760 us; the launch traced here: 758 us
  waiting for transfers between devices  532 us (70%)
  starting transfers between devices  109 us (14%)
  Pallas kernels  45.6 us (6%)
  other arithmetic  37.9 us (5%)
  between operations  19.9 us (3%)
  local copies, waits for them, and re-layouts  12.7 us (2%)
    psum x4, waiting for transfers between devices, on_device(): total = lax.psum(sums, ('row', 'col'))  449 us
    ppermute x32, starting transfers between devices, shifted(): lax.ppermute(value, axis, [(source, source + steps) for source in range(l...  109 us
    ppermute x32, waiting for transfers between devices, shifted(): lax.ppermute(value, axis, [(source, source + steps) for source in range(l...  83.3 us
    pallas_call x4, Pallas kernels, batch_sums(): pl.pallas_call(batch_kernel, out_shape=(jax.ShapeDtypeStruct(extended.sha...  45.6 us
  transfers between devices with their start and end apart: 36, of which 26 were waited for; matrix products, arithmetic and copies ran while one was open for 4% of the time, Pallas kernels for 0%

commit v1 on v0

--- a/solution.py
+++ b/solution.py
@@ -191,13 +191,13 @@
                 magnitudes[0, 0, batch], forward, inverse,
             )
             probe_peak = jnp.max(jnp.sum(probe * probe, axis=(0, 1))) + tiny_value
-            total = lax.psum(sums, ("row", "col"))
+            tail = 2 * modes * side
+            scalars = lax.psum(jnp.sum(sums[tail : tail + 2], axis=1), ("row", "col"))
+            summed = lax.psum(sums[:tail].reshape(probe.shape), ("row", "col"))
             interior = return_rims(object_grad, margin)
             object_field = object_field + object_rate / probe_peak * interior
-            tail = 2 * modes * side
-            power_total = jnp.sum(total[tail])
-            errors.append(jnp.sum(total[tail + 1]))
-            summed = total[:tail].reshape(probe.shape)
+            power_total = scalars[0]
+            errors.append(scalars[1])
             probe = probe + probe_rate * side * side / power_total * summed
     return (object_field, probe, jnp.stack(errors))
 

time: 760 us -> 757 us (level)
  blocking collectives: 0 us -> 187 us
  waiting for transfers between devices: 532 us -> 345 us
  local copies, waits for them, and re-layouts: 12.7 us -> 29 us
  Pallas kernels: 45.6 us -> 32.1 us
  starting transfers between devices: 109 us -> 100 us
    psum x0 -> x4, blocking collectives: none -> 187 us  [on_device(): scalars = lax.psum(jnp.sum(sums[tail:tail + 2], axis=1), ('row', 'col'))]
    psum x4, waiting for transfers between devices: 449 us -> 279 us  [on_device(): summed = lax.psum(sums[:tail].reshape(probe.shape), ('row', 'col'))]
    ppermute x32, waiting for transfers between devices: 83.3 us -> 65.4 us  [shifted(): lax.ppermute(value, axis, [(source, source + steps) for source in range(l...]
    pallas_call x4, Pallas kernels: 45.6 us -> 32.1 us  [batch_sums(): pl.pallas_call(batch_kernel, out_shape=(jax.ShapeDtypeStruct(extended.sha...]
    slice x0 -> x8, local copies, waits for them, and re-layouts: none -> 11.7 us  [the longest x4 9.16 us: on_device(): summed = lax.psum(sums[:tail].reshape(probe.shape), ('row', 'col'))]
    ppermute x32, starting transfers between devices: 109 us -> 100 us  [shifted(): lax.ppermute(value, axis, [(source, source + steps) for source in range(l...]
  transfers between devices with their start and end apart: 36 -> 36, of which waited for: 26 -> 19; matrix products, arithmetic and copies ran while one was open for 4% -> 6% of each run, Pallas kernels for 0% -> 0%
where the time goes in v1:
time: 757 us; the launch traced here: 752 us
  waiting for transfers between devices  345 us (46%)
  blocking collectives  187 us (25%)
  starting transfers between devices  100 us (13%)
  other arithmetic  38.1 us (5%)
  Pallas kernels  32.1 us (4%)
  local copies, waits for them, and re-layouts  29 us (4%)
  between operations  20.2 us (3%)
    psum x4, waiting for transfers between devices, on_device(): summed = lax.psum(sums[:tail].reshape(probe.shape), ('row', 'col'))  279 us
    psum x4, blocking collectives, on_device(): scalars = lax.psum(jnp.sum(sums[tail:tail + 2], axis=1), ('row', 'col'))  187 us
    ppermute x32, starting transfers between devices, shifted(): lax.ppermute(value, axis, [(source, source + steps) for source in range(l...  100 us
    ppermute x32, waiting for transfers between devices, shifted(): lax.ppermute(value, axis, [(source, source + steps) for source in range(l...  65.4 us
    pallas_call x4, Pallas kernels, batch_sums(): pl.pallas_call(batch_kernel, out_shape=(jax.ShapeDtypeStruct(extended.sha...  32.1 us
  transfers between devices with their start and end apart: 36, of which 19 were waited for; matrix products, arithmetic and copies ran while one was open for 6% of the time, Pallas kernels for 0%

profile of v1, /device:TPU:0, one launch (start us, length us, event | category | flops | bytes accessed | tf_op | source)
XLA Modules:
  0.0 751.7 jit_solution(4404065133769983155)
XLA Ops:
  8.3 4.9 collective-permute-start
  13.2 1.4 collective-permute-start.1
  14.7 4.1 collective-permute-done
  19.8 6.5 collective-permute-done.1
  29.8 3.4 collective-permute-done.3
  33.5 10.1 %shard_map.103 = (f32[2,512,512]{2,1,0:T(8,128)S(1)}, f32[2056,256]{1,0:T(8,128)S(1)}) custom-call(s32[3]{0:T(128)S(1)} %get-tuple-element.74.rows_ref, s32[3]{0:T(128)S(1)} %get-tuple-element.61.cols_ref, s32[1]{0:T(128)} %bitcast.2.count_ref, f32[2,512,512]{2,1,0:T(8,128)S(1)} %pad_maximum_fusion.ext_ref, f32[2,4,256,256]{3,2,1,0:T(8,128)S(1)} %copy-done.2, ...), custom_call_target="tpu_custom_call" | custom-call | flops 12884901888 | bytes 10485760 | tf_op jit(solution)/shard_map/pallas_call | solution.py:153
  43.7 1.6 slice.216
  46.8 5.5 collective-permute-start.4
  54.4 48.0 %psum.56 = f32[2]{0:T(128)S(1)} all-reduce(f32[2]{0:T(128)S(1)} %slice_reduce_fusion.3), channel_id=1, replica_groups=mesh['row'=4,'col'=8] {'row','col'}, use_global_device_ids=true, to_apply=%region_3.0 | all-reduce | flops 2 | bytes 16 | tf_op jit(solution)/shard_map/psum | solution.py:195
  103.7 1.4 maximum_add_fusion
  106.9 4.9 collective-permute-start.6
  113.1 79.4 %all-reduce.5.cloned.1.call-done = f32[2,4,256,256]{3,2,1,0:T(8,128)} async-done(((f32[2,4,256,256]{3,2,1,0:T(8,128)}), f32[2,4,256,256]{3,2,1,0:T(8,128)}) %all-reduce.5.cloned.1.call-update) | async-done | bytes 2097168 | tf_op jit(solution)/shard_map/psum | solution.py:196
  192.5 3.5 multiply_reduce_fusion.2
  196.0 1.7 reduce_max.36
  198.4 1.4 fusion.7
  199.9 3.2 collective-permute-start.8
  204.4 3.2 collective-permute-done.8
  207.6 7.5 collective-permute-done.9
  215.3 1.3 collective-permute-start.10
  216.6 1.4 collective-permute-start.11
  218.1 3.6 collective-permute-done.11
  221.9 6.0 shard_map.104
  228.0 17.9 %collective-permute-start.12 = (f32[2,512,128]{2,1,0:T(8,128)S(1)}, f32[2,512,128]{2,1,0:T(8,128)S(1)}, u32[]{:S(2)}, u32[]{:S(2)}) collective-permute-start(f32[2,512,128]{2,1,0:T(8,128)S(1)} %get-tuple-element.29), channel_id=1, source_target_pairs={{0,1},{1,2},{2,3},{3,4},{4,5},{5,6},{6,7},{8,9},{9,10},{10,11},{11... | collective-permute-start | bytes 1572872 | tf_op jit(solution)/shard_map/ppermute | solution.py:29
  247.4 2.3 collective-permute-done.13
  251.1 2.0 collective-permute-start.14
  254.4 1.7 reduce_max.37
  256.8 3.0 slice.233
  259.9 2.8 collective-permute-done.15
  262.8 1.4 fusion.5
  264.3 2.3 collective-permute-start.16
  267.9 2.7 collective-permute-done.16
  270.6 9.1 %collective-permute-done.17 = f32[2,128,256]{2,1,0:T(8,128)S(1)} collective-permute-done((f32[2,128,256]{2,1,0:T(8,128)S(1)}, f32[2,128,256]{2,1,0:T(8,128)S(1)}, u32[]{:S(2)}, u32[]{:S(2)}) %collective-permute-start.17) | collective-permute-done | bytes 262176 | tf_op jit(solution)/shard_map/ppermute | solution.py:29
  280.8 6.8 collective-permute-start.18
  289.8 46.2 %psum.58 = f32[2]{0:T(128)S(1)} all-reduce(f32[2]{0:T(128)S(1)} %slice_reduce_fusion.2), channel_id=1, replica_groups=mesh['row'=4,'col'=8] {'row','col'}, use_global_device_ids=true, to_apply=%region_8.0 | all-reduce | flops 2 | bytes 16 | tf_op jit(solution)/shard_map/psum | solution.py:195
  337.3 63.1 %all-reduce.7.cloned.1.call-done = f32[2,4,256,256]{3,2,1,0:T(8,128)} async-done(((f32[2,4,256,256]{3,2,1,0:T(8,128)}), f32[2,4,256,256]{3,2,1,0:T(8,128)}) %all-reduce.7.cloned.1.call-update) | async-done | bytes 2097168 | tf_op jit(solution)/shard_map/psum | solution.py:196
  400.4 2.7 multiply_reduce_fusion.1
  403.1 2.2 pad_maximum_fusion.2.ext_ref
  405.4 10.1 %shard_map.105 = (f32[2,512,512]{2,1,0:T(8,128)S(1)}, f32[2056,256]{1,0:T(8,128)S(1)}) custom-call(s32[3]{0:T(128)S(1)} %get-tuple-element.74.rows_ref, s32[3]{0:T(128)S(1)} %get-tuple-element.61.cols_ref, s32[1]{0:T(128)} %bitcast.2.count_ref, f32[2,512,512]{2,1,0:T(8,128)S(1)} %pad_maximum_fusion.2.ext_ref, ...), custom_call_target="tpu_custom_call" | custom-call | flops 12884901888 | bytes 10485760 | tf_op jit(solution)/shard_map/pallas_call | solution.py:153
  417.0 1.5 collective-permute-start.21
  418.5 3.7 collective-permute-done.21
  424.2 2.5 collective-permute-start.22
  428.0 1.7 reduce_max.38
  430.4 1.5 slice.246
  432.0 4.5 collective-permute-done.23
  436.4 1.4 fusion.3
  437.9 4.8 collective-permute-start.24
  444.0 4.0 collective-permute-done.24
  448.0 7.8 %collective-permute-done.25 = f32[2,128,256]{2,1,0:T(8,128)S(1)} collective-permute-done((f32[2,128,256]{2,1,0:T(8,128)S(1)}, f32[2,128,256]{2,1,0:T(8,128)S(1)}, u32[]{:S(2)}, u32[]{:S(2)}) %collective-permute-start.25) | collective-permute-done | bytes 262176 | tf_op jit(solution)/shard_map/ppermute | solution.py:29
  456.9 7.1 collective-permute-start.26
  465.5 45.3 %psum.60 = f32[2]{0:T(128)S(1)} all-reduce(f32[2]{0:T(128)S(1)} %slice_reduce_fusion.1), channel_id=1, replica_groups=mesh['row'=4,'col'=8] {'row','col'}, use_global_device_ids=true, to_apply=%region_13.0 | all-reduce | flops 2 | bytes 16 | tf_op jit(solution)/shard_map/psum | solution.py:195
  512.1 63.9 %all-reduce.9.cloned.1.call-done = f32[2,4,256,256]{3,2,1,0:T(8,128)} async-done(((f32[2,4,256,256]{3,2,1,0:T(8,128)}), f32[2,4,256,256]{3,2,1,0:T(8,128)}) %all-reduce.9.cloned.1.call-update) | async-done | bytes 2097168 | tf_op jit(solution)/shard_map/psum | solution.py:196
  576.0 3.4 multiply_reduce_fusion
  579.5 1.5 pad_maximum_fusion.3.ext_ref
  581.0 5.8 shard_map.106
  586.8 1.3 copy-done.4
  590.5 9.3 %collective-permute-start.28 = (f32[2,512,128]{2,1,0:T(8,128)}, f32[2,512,128]{2,1,0:T(8,128)S(1)}, u32[]{:S(2)}, u32[]{:S(2)}) collective-permute-start(f32[2,512,128]{2,1,0:T(8,128)} %get-tuple-element.25), channel_id=1, source_target_pairs={{0,1},{1,2},{2,3},{3,4},{4,5},{5,6},{6,7},{8,9},{9,10},{10,11},{11... | collective-permute-start | bytes 1572872 | tf_op jit(solution)/shard_map/ppermute | solution.py:29
  602.5 3.1 slice.259
  605.6 1.5 maximum_add_fusion.3
  608.9 4.0 collective-permute-start.30
  615.0 47.7 %psum.62 = f32[2]{0:T(128)S(1)} all-reduce(f32[2]{0:T(128)S(1)} %slice_reduce_fusion), channel_id=1, replica_groups=mesh['row'=4,'col'=8] {'row','col'}, use_global_device_ids=true, to_apply=%region_18.0 | all-reduce | flops 2 | bytes 16 | tf_op jit(solution)/shard_map/psum | solution.py:195
  664.0 3.1 pad_maximum_fusion.7
  667.2 1.9 fusion.1
  669.1 72.9 %all-reduce.11.cloned.1.call-done = f32[2,4,256,256]{3,2,1,0:T(8,128)} async-done(((f32[2,4,256,256]{3,2,1,0:T(8,128)}), f32[2,4,256,256]{3,2,1,0:T(8,128)}) %all-reduce.11.cloned.1.call-update) | async-done | bytes 2097168 | tf_op jit(solution)/shard_map/psum | solution.py:196
  742.0 3.2 multiply_add_fusion
  (150 shorter events, 42.5 us)
Async XLA Ops:
  7.2 185.3 %all-reduce.5.cloned.1.call-start = ((), (), s32[]{:S(2)}) async-start(), calls=%async_computation | async-start | bytes 4194304 | tf_op jit(solution)/shard_map/psum | solution.py:196
  8.3 10.4 %collective-permute-start = (f32[2,128,256]{2,1,0:T(8,128)S(1)}, f32[2,128,256]{2,1,0:T(8,128)S(1)}, u32[]{:S(2)}, u32[]{:S(2)}) collective-permute-start(f32[2,128,256]{2,1,0:T(8,128)S(1)} %get-tuple-element.59), channel_id=1, source_target_pairs={{0,8},{8,16},{16,24},{1,9},{9,17},{17,25},{2,10},{10,18},{18,26},{... | collective-permute-start | bytes 786440 | tf_op jit(solution)/shard_map/ppermute | solution.py:29
  13.2 15.8 %copy-start.33 = (s32[1,1,2]{2,1,0:T(1,128)S(1)}, s32[1,1,2]{2,1,0:T(1,128)}, u32[]{:S(2)}) copy-start(s32[1,1,2]{2,1,0:T(1,128)} %param.12) | copy-start | bytes 28
  13.2 16.4 %copy-start.34 = (s32[1,1,2,3]{3,2,1,0:T(2,128)S(1)}, s32[1,1,2,3]{3,2,1,0:T(2,128)}, u32[]{:S(2)}) copy-start(s32[1,1,2,3]{3,2,1,0:T(2,128)} %param.11) | copy-start | bytes 76
  13.2 16.4 %copy-start.35 = (s32[1,1,2,3]{3,2,1,0:T(2,128)S(1)}, s32[1,1,2,3]{3,2,1,0:T(2,128)}, u32[]{:S(2)}) copy-start(s32[1,1,2,3]{3,2,1,0:T(2,128)} %param.10) | copy-start | bytes 76
  13.2 16.4 %copy-start.23 = (f32[1,1,2,3,256,256]{5,4,3,2,1,0:T(8,128)S(1)}, f32[1,1,2,3,256,256]{5,4,3,2,1,0:T(8,128)}, u32[]{:S(2)}) copy-start(f32[1,1,2,3,256,256]{5,4,3,2,1,0:T(8,128)} %param.13) | copy-start | bytes 4718596
  13.2 13.0 %collective-permute-start.1 = (f32[2,128,256]{2,1,0:T(8,128)S(1)}, f32[2,128,256]{2,1,0:T(8,128)S(1)}, u32[]{:S(2)}, u32[]{:S(2)}) collective-permute-start(f32[2,128,256]{2,1,0:T(8,128)S(1)} %get-tuple-element.58), channel_id=1, source_target_pairs={{8,0},{16,8},{24,16},{9,1},{17,9},{25,17},{10,2},{18,10},{26,18},{... | collective-permute-start | bytes 786440 | tf_op jit(solution)/shard_map/ppermute | solution.py:29
  26.4 3.5 collective-permute-start.2
  27.7 5.6 collective-permute-start.3
  29.8 3.7 copy-start.6
  29.8 3.7 copy-start.2
  29.8 3.7 copy-start.8
  29.8 3.7 copy-start.9
  43.7 2.0 copy-start.5
  45.7 354.7 %all-reduce.7.cloned.1.call-start = ((), (), s32[]{:S(2)}) async-start(), calls=%async_computation.1 | async-start | bytes 4194304 | tf_op jit(solution)/shard_map/psum | solution.py:196
  46.8 56.9 %collective-permute-start.4 = (f32[2,512,128]{2,1,0:T(8,128)}, f32[2,512,128]{2,1,0:T(8,128)}, u32[]{:S(2)}, u32[]{:S(2)}) collective-permute-start(f32[2,512,128]{2,1,0:T(8,128)} %get-tuple-element.32), channel_id=1, source_target_pairs={{0,1},{1,2},{2,3},{3,4},{4,5},{5,6},{6,7},{8,9},{9,10},{10,11},{11... | collective-permute-start | bytes 1572872 | tf_op jit(solution)/shard_map/ppermute | solution.py:29
  52.3 51.4 %collective-permute-start.5 = (f32[2,512,128]{2,1,0:T(8,128)}, f32[2,512,128]{2,1,0:T(8,128)}, u32[]{:S(2)}, u32[]{:S(2)}) collective-permute-start(f32[2,512,128]{2,1,0:T(8,128)} %get-tuple-element.33), channel_id=1, source_target_pairs={{1,0},{2,1},{3,2},{4,3},{5,4},{6,5},{7,6},{9,8},{10,9},{11,10},{12... | collective-permute-start | bytes 1572872 | tf_op jit(solution)/shard_map/ppermute | solution.py:29
  106.9 91.5 %collective-permute-start.6 = (f32[2,128,256]{2,1,0:T(8,128)}, f32[2,128,256]{2,1,0:T(8,128)}, u32[]{:S(2)}, u32[]{:S(2)}) collective-permute-start(f32[2,128,256]{2,1,0:T(8,128)} %get-tuple-element.48), channel_id=1, source_target_pairs={{0,8},{8,16},{16,24},{1,9},{9,17},{17,25},{2,10},{10,18},{18,26},{... | collective-permute-start | bytes 786440 | tf_op jit(solution)/shard_map/ppermute | solution.py:29
  111.8 86.6 %collective-permute-start.7 = (f32[2,128,256]{2,1,0:T(8,128)}, f32[2,128,256]{2,1,0:T(8,128)}, u32[]{:S(2)}, u32[]{:S(2)}) collective-permute-start(f32[2,128,256]{2,1,0:T(8,128)} %get-tuple-element.49), channel_id=1, source_target_pairs={{8,0},{16,8},{24,16},{9,1},{17,9},{25,17},{10,2},{18,10},{26,18},{... | collective-permute-start | bytes 786440 | tf_op jit(solution)/shard_map/ppermute | solution.py:29
  199.8 21.9 %copy-start.18 = (f32[2,256,256]{2,1,0:T(8,128)}, f32[2,256,256]{2,1,0:T(8,128)S(1)}, u32[]{:S(2)}) copy-start(f32[2,256,256]{2,1,0:T(8,128)S(1)} %fusion.7) | copy-start | bytes 1572868
  199.9 7.7 %collective-permute-start.8 = (f32[2,128,256]{2,1,0:T(8,128)S(1)}, f32[2,128,256]{2,1,0:T(8,128)S(1)}, u32[]{:S(2)}, u32[]{:S(2)}) collective-permute-start(f32[2,128,256]{2,1,0:T(8,128)S(1)} %get-tuple-element.56), channel_id=1, source_target_pairs={{0,8},{8,16},{16,24},{1,9},{9,17},{17,25},{2,10},{10,18},{18,26},{... | collective-permute-start | bytes 786440 | tf_op jit(solution)/shard_map/ppermute | solution.py:29
  203.1 12.0 %collective-permute-start.9 = (f32[2,128,256]{2,1,0:T(8,128)S(1)}, f32[2,128,256]{2,1,0:T(8,128)S(1)}, u32[]{:S(2)}, u32[]{:S(2)}) collective-permute-start(f32[2,128,256]{2,1,0:T(8,128)S(1)} %get-tuple-element.57), channel_id=1, source_target_pairs={{8,0},{16,8},{24,16},{9,1},{17,9},{25,17},{10,2},{18,10},{26,18},{... | collective-permute-start | bytes 786440 | tf_op jit(solution)/shard_map/ppermute | solution.py:29
  215.3 2.8 collective-permute-start.10
  216.6 5.3 copy-start.10
  216.6 5.1 collective-permute-start.11
  228.0 22.0 %copy-start.3 = (f32[2056,256]{1,0:T(8,128)}, f32[2056,256]{1,0:T(8,128)S(1)}, u32[]{:S(2)}) copy-start(f32[2056,256]{1,0:T(8,128)S(1)} %get-tuple-element.14) | copy-start | bytes 6316036
  228.0 19.4 %collective-permute-start.12 = (f32[2,512,128]{2,1,0:T(8,128)S(1)}, f32[2,512,128]{2,1,0:T(8,128)S(1)}, u32[]{:S(2)}, u32[]{:S(2)}) collective-permute-start(f32[2,512,128]{2,1,0:T(8,128)S(1)} %get-tuple-element.29), channel_id=1, source_target_pairs={{0,1},{1,2},{2,3},{3,4},{4,5},{5,6},{6,7},{8,9},{9,10},{10,11},{11... | collective-permute-start | bytes 1572872 | tf_op jit(solution)/shard_map/ppermute | solution.py:29
  245.9 3.8 collective-permute-start.13
  251.1 8.8 %collective-permute-start.14 = (f32[2,128,256]{2,1,0:T(8,128)}, f32[2,128,256]{2,1,0:T(8,128)}, u32[]{:S(2)}, u32[]{:S(2)}) collective-permute-start(f32[2,128,256]{2,1,0:T(8,128)} %get-tuple-element.44), channel_id=1, source_target_pairs={{0,8},{8,16},{16,24},{1,9},{9,17},{17,25},{2,10},{10,18},{18,26},{... | collective-permute-start | bytes 786440 | tf_op jit(solution)/shard_map/ppermute | solution.py:29
  253.1 9.6 %collective-permute-start.15 = (f32[2,128,256]{2,1,0:T(8,128)}, f32[2,128,256]{2,1,0:T(8,128)}, u32[]{:S(2)}, u32[]{:S(2)}) collective-permute-start(f32[2,128,256]{2,1,0:T(8,128)} %get-tuple-element.45), channel_id=1, source_target_pairs={{8,0},{16,8},{24,16},{9,1},{17,9},{25,17},{10,2},{18,10},{26,18},{... | collective-permute-start | bytes 786440 | tf_op jit(solution)/shard_map/ppermute | solution.py:29
  259.9 316.1 %all-reduce.9.cloned.1.call-start = ((), (), s32[]{:S(2)}) async-start(), calls=%async_computation.2 | async-start | bytes 4194304 | tf_op jit(solution)/shard_map/psum | solution.py:196
  264.2 16.6 %copy-start.16 = (f32[2,256,256]{2,1,0:T(8,128)}, f32[2,256,256]{2,1,0:T(8,128)S(1)}, u32[]{:S(2)}) copy-start(f32[2,256,256]{2,1,0:T(8,128)S(1)} %fusion.5) | copy-start | bytes 1572868
  264.3 6.3 collective-permute-start.16
  266.6 13.1 %collective-permute-start.17 = (f32[2,128,256]{2,1,0:T(8,128)S(1)}, f32[2,128,256]{2,1,0:T(8,128)S(1)}, u32[]{:S(2)}, u32[]{:S(2)}) collective-permute-start(f32[2,128,256]{2,1,0:T(8,128)S(1)} %get-tuple-element.55), channel_id=1, source_target_pairs={{8,0},{16,8},{24,16},{9,1},{17,9},{25,17},{10,2},{18,10},{26,18},{... | collective-permute-start | bytes 786440 | tf_op jit(solution)/shard_map/ppermute | solution.py:29
  270.6 10.3 %copy-start.24 = (f32[2,128,256]{2,1,0:T(8,128)}, f32[2,128,256]{2,1,0:T(8,128)S(1)}, u32[]{:S(2)}) copy-start(f32[2,128,256]{2,1,0:T(8,128)S(1)} %collective-permute-done.16) | copy-start | bytes 786436
  280.8 122.3 %collective-permute-start.18 = (f32[2,512,128]{2,1,0:T(8,128)}, f32[2,512,128]{2,1,0:T(8,128)}, u32[]{:S(2)}, u32[]{:S(2)}) collective-permute-start(f32[2,512,128]{2,1,0:T(8,128)} %get-tuple-element.42), channel_id=1, source_target_pairs={{0,1},{1,2},{2,3},{3,4},{4,5},{5,6},{6,7},{8,9},{9,10},{10,11},{11... | collective-permute-start | bytes 1572872 | tf_op jit(solution)/shard_map/ppermute | solution.py:29
  287.7 115.4 %collective-permute-start.19 = (f32[2,512,128]{2,1,0:T(8,128)}, f32[2,512,128]{2,1,0:T(8,128)}, u32[]{:S(2)}, u32[]{:S(2)}) collective-permute-start(f32[2,512,128]{2,1,0:T(8,128)} %get-tuple-element.43), channel_id=1, source_target_pairs={{1,0},{2,1},{3,2},{4,3},{5,4},{6,5},{7,6},{9,8},{10,9},{11,10},{12... | collective-permute-start | bytes 1572872 | tf_op jit(solution)/shard_map/ppermute | solution.py:29
  400.4 2.7 copy-start.17
  400.4 2.8 copy-start.25
  400.4 2.8 copy-start.29
  403.1 2.3 copy-start
  403.1 2.3 copy-start.7
  403.1 2.3 copy-start.11
  415.6 2.9 collective-permute-start.20
  417.0 5.2 collective-permute-start.21
  424.2 7.8 %collective-permute-start.22 = (f32[2,128,256]{2,1,0:T(8,128)}, f32[2,128,256]{2,1,0:T(8,128)}, u32[]{:S(2)}, u32[]{:S(2)}) collective-permute-start(f32[2,128,256]{2,1,0:T(8,128)} %get-tuple-element.40), channel_id=1, source_target_pairs={{0,8},{8,16},{16,24},{1,9},{9,17},{17,25},{2,10},{10,18},{18,26},{... | collective-permute-start | bytes 786440 | tf_op jit(solution)/shard_map/ppermute | solution.py:29
  426.7 9.8 %collective-permute-start.23 = (f32[2,128,256]{2,1,0:T(8,128)}, f32[2,128,256]{2,1,0:T(8,128)}, u32[]{:S(2)}, u32[]{:S(2)}) collective-permute-start(f32[2,128,256]{2,1,0:T(8,128)} %get-tuple-element.41), channel_id=1, source_target_pairs={{8,0},{16,8},{24,16},{9,1},{17,9},{25,17},{10,2},{18,10},{26,18},{... | collective-permute-start | bytes 786440 | tf_op jit(solution)/shard_map/ppermute | solution.py:29
  431.9 310.1 %all-reduce.11.cloned.1.call-start = ((), (), s32[]{:S(2)}) async-start(), calls=%async_computation.3 | async-start | bytes 4194304 | tf_op jit(solution)/shard_map/psum | solution.py:196
  437.9 19.0 %copy-start.13 = (f32[2,256,256]{2,1,0:T(8,128)}, f32[2,256,256]{2,1,0:T(8,128)S(1)}, u32[]{:S(2)}) copy-start(f32[2,256,256]{2,1,0:T(8,128)S(1)} %fusion.3) | copy-start | bytes 1572868
  437.9 10.0 %collective-permute-start.24 = (f32[2,128,256]{2,1,0:T(8,128)S(1)}, f32[2,128,256]{2,1,0:T(8,128)S(1)}, u32[]{:S(2)}, u32[]{:S(2)}) collective-permute-start(f32[2,128,256]{2,1,0:T(8,128)S(1)} %get-tuple-element.52), channel_id=1, source_target_pairs={{0,8},{8,16},{16,24},{1,9},{9,17},{17,25},{2,10},{10,18},{18,26},{... | collective-permute-start | bytes 786440 | tf_op jit(solution)/shard_map/ppermute | solution.py:29
  442.7 13.1 %collective-permute-start.25 = (f32[2,128,256]{2,1,0:T(8,128)S(1)}, f32[2,128,256]{2,1,0:T(8,128)S(1)}, u32[]{:S(2)}, u32[]{:S(2)}) collective-permute-start(f32[2,128,256]{2,1,0:T(8,128)S(1)} %get-tuple-element.53), channel_id=1, source_target_pairs={{8,0},{16,8},{24,16},{9,1},{17,9},{25,17},{10,2},{18,10},{26,18},{... | collective-permute-start | bytes 786440 | tf_op jit(solution)/shard_map/ppermute | solution.py:29
  448.0 9.0 %copy-start.26 = (f32[2,128,256]{2,1,0:T(8,128)}, f32[2,128,256]{2,1,0:T(8,128)S(1)}, u32[]{:S(2)}) copy-start(f32[2,128,256]{2,1,0:T(8,128)S(1)} %collective-permute-done.24) | copy-start | bytes 786436
  456.9 122.5 %collective-permute-start.26 = (f32[2,512,128]{2,1,0:T(8,128)}, f32[2,512,128]{2,1,0:T(8,128)}, u32[]{:S(2)}, u32[]{:S(2)}) collective-permute-start(f32[2,512,128]{2,1,0:T(8,128)} %get-tuple-element.38), channel_id=1, source_target_pairs={{0,1},{1,2},{2,3},{3,4},{4,5},{5,6},{6,7},{8,9},{9,10},{10,11},{11... | collective-permute-start | bytes 1572872 | tf_op jit(solution)/shard_map/ppermute | solution.py:29
  464.1 115.4 %collective-permute-start.27 = (f32[2,512,128]{2,1,0:T(8,128)}, f32[2,512,128]{2,1,0:T(8,128)}, u32[]{:S(2)}, u32[]{:S(2)}) collective-permute-start(f32[2,512,128]{2,1,0:T(8,128)} %get-tuple-element.39), channel_id=1, source_target_pairs={{1,0},{2,1},{3,2},{4,3},{5,4},{6,5},{7,6},{9,8},{10,9},{11,10},{12... | collective-permute-start | bytes 1572872 | tf_op jit(solution)/shard_map/ppermute | solution.py:29
  576.0 3.4 copy-start.14
  576.0 3.5 copy-start.27
  576.0 3.5 copy-start.31
  579.5 1.5 copy-start.12
  588.2 13.0 %copy-start.32 = (f32[256,256]{1,0:T(8,128)S(1)}, f32[256,256]{1,0:T(8,128)}, u32[]{:S(2)}) copy-start(f32[256,256]{1,0:T(8,128)} %get-tuple-element.19) | copy-start | bytes 786436
  590.5 15.1 %collective-permute-start.28 = (f32[2,512,128]{2,1,0:T(8,128)}, f32[2,512,128]{2,1,0:T(8,128)S(1)}, u32[]{:S(2)}, u32[]{:S(2)}) collective-permute-start(f32[2,512,128]{2,1,0:T(8,128)} %get-tuple-element.25), channel_id=1, source_target_pairs={{0,1},{1,2},{2,3},{3,4},{4,5},{5,6},{6,7},{8,9},{9,10},{10,11},{11... | collective-permute-start | bytes 1572872 | tf_op jit(solution)/shard_map/ppermute | solution.py:29
  599.8 5.8 collective-permute-start.29
  605.6 61.6 %copy-start.15 = (f32[2,256,256]{2,1,0:T(8,128)S(1)}, f32[2,256,256]{2,1,0:T(8,128)}, u32[]{:S(2)}) copy-start(f32[2,256,256]{2,1,0:T(8,128)} %copy-done.13) | copy-start | bytes 1572868
  608.9 58.3 %collective-permute-start.30 = (f32[2,128,256]{2,1,0:T(8,128)}, f32[2,128,256]{2,1,0:T(8,128)S(1)}, u32[]{:S(2)}, u32[]{:S(2)}) collective-permute-start(f32[2,128,256]{2,1,0:T(8,128)} %get-tuple-element.36), channel_id=1, source_target_pairs={{0,8},{8,16},{16,24},{1,9},{9,17},{17,25},{2,10},{10,18},{18,26},{... | collective-permute-start | bytes 786440 | tf_op jit(solution)/shard_map/ppermute | solution.py:29
  612.9 54.3 %collective-permute-start.31 = (f32[2,128,256]{2,1,0:T(8,128)S(1)}, f32[2,128,256]{2,1,0:T(8,128)S(1)}, u32[]{:S(2)}, u32[]{:S(2)}) collective-permute-start(f32[2,128,256]{2,1,0:T(8,128)S(1)} %get-tuple-element.37), channel_id=1, source_target_pairs={{8,0},{16,8},{24,16},{9,1},{17,9},{25,17},{10,2},{18,10},{26,18},{... | collective-permute-start | bytes 786440 | tf_op jit(solution)/shard_map/ppermute | solution.py:29
  (8 other events, 9.1 us)
Sparse Core Ops, SparseCore 0:
  45.8 146.6 all-reduce.4
  260.0 140.3 all-reduce.6
  432.0 143.9 all-reduce.8
  605.7 136.2 all-reduce.10
